TPU v7x, 32 devices: a whole 2x2x4 slice. The times are simulated.
32 devices in a mesh: member: 8 (over z, y), band: 4 (over x, core).
Axes of the slice: x: 2, y: 2, z: 4, core: 2. Of those that a mesh axis runs over, the one named last changes fastest.
Arguments:
- spectral: float32 [128, 768, 768], P('member', 'band'), parts along dimension 0, may hold values from -6 to 6
- coupling: float32 [8192, 1024], P(('member', 'band')), parts along dimension 0, may hold values from 0.02 to 162, as said below
- quadratic: float32 [8192, 1024], P(('member', 'band')), parts along dimension 0, may hold values from -1.5 to 1.5
Outputs:
- tendency_spectral: float32 [128, 768, 768], P('member', 'band'), parts along dimension 0
There are 8 independent parts, one for each index of `member`. A program takes and returns all parts, laid end to end along the dimension named above; each array names one. Nothing has to cross between parts.
Inputs may be any that keep to these rules, and one draw needn't show every extreme that they name: `coupling`: positive.
All inputs are finite; a program needn't handle non-finite values.
Results may differ from a plain program's by a relative error of at most 0.00008.
Values sent between devices are 32-bit elements; how exact they have to be, the bound alone decides.
A program may use at most 128 MiB of HBM per device.

v0:
```python
import math

import jax
import jax.numpy as jnp
from jax import lax
from jax.sharding import PartitionSpec as P


def tables(cells, coeffs):
    half_count = coeffs // 2
    position = jnp.arange(cells, dtype=jnp.int32)
    column = jnp.arange(coeffs, dtype=jnp.int32)
    wavenumber = jnp.where(column < half_count, column, column - half_count)
    turns = position[:, None] * wavenumber[None, :] % cells
    angles = turns.astype(jnp.float32) * (2.0 * math.pi / cells)
    basis_table = jnp.where(column[None, :] < half_count, jnp.cos(angles), jnp.sin(angles))
    synthesis = basis_table / math.sqrt(half_count)
    factor = jnp.where(wavenumber == 0, 1.0, 2.0) * (math.sqrt(half_count) / cells)
    analysis = (basis_table * factor[None, :]).T
    return (synthesis, analysis)


def on_device(spectral, coupling, quadratic):
    high = lax.Precision.HIGH
    levels, band, coeffs = spectral.shape
    cells = coupling.shape[1]
    ways = lax.axis_size("band")
    synthesis, analysis = tables(cells, coeffs)
    points = float(cells * cells)

    arrived = [
        lax.all_to_all(spectral[at : at + ways], "band", split_axis=0, concat_axis=0, tiled=True)
        for at in range(0, levels, ways)
    ]
    coupling = lax.all_gather(coupling, "band", axis=0, tiled=True)
    quadratic = lax.all_gather(quadratic, "band", axis=0, tiled=True)
    outputs = []
    for field in arrived:
        field = field.reshape(coeffs, coeffs)
        section = jnp.einsum("xa,ab->xb", synthesis, field, precision=high)
        grid = jnp.einsum("yb,xb->yx", synthesis, section, precision=high)
        product = coupling * grid
        energy = jnp.sum(product * product) / points
        scaled = product * (1.0 / jnp.sqrt(energy + 1e-06))
        tendency = scaled + quadratic * scaled * scaled
        back = jnp.einsum("ax,yx->ay", analysis, tendency, precision=high)
        done = jnp.einsum("ay,by->ab", back, analysis, precision=high)
        done = done.reshape(ways, band, coeffs)
        outputs.append(lax.all_to_all(done, "band", split_axis=0, concat_axis=0, tiled=True))
    return jnp.concatenate(outputs, axis=0)


def solution(mesh):
    placed = (P("member", "band", None), P(("member", "band"), None), P(("member", "band"), None))
    return jax.shard_map(
        on_device, mesh=mesh, in_specs=placed, out_specs=P("member", "band", None), check_vma=False
    )
```

profile of v0, /device:TPU:0, one launch (start us, length us, event | category | flops | bytes accessed | tf_op | source)
XLA Modules:
  0.0 557.4 jit_solution(15243473083543496365)
XLA Ops:
  6.5 0.0 all-gather.3.cloned.1.call-start
  6.5 0.7 all-gather.3.cloned.1.call-update
  7.3 6.8 %fusion.130 = (f32[4,192,768]{2,1,0:T(8,128)S(1)}, f32[4,192,768]{2,1,0:T(8,128)}, f32[4,192,768]{2,1,0:T(8,128)}, f32[4,192,768]{2,1,0:T(8,128)}) fusion(f32[16,192,768]{2,1,0:T(8,128)} %param.3), kind=kLoop, calls=%fused_computation.150 | loop fusion | bytes 18874368 | tf_op jit(solution)/shard_map/slice | solution.py:32
  14.1 55.0 %all_to_all.40 = f32[4,192,768]{2,1,0:T(8,128)S(1)} all-to-all(f32[4,192,768]{2,1,0:T(8,128)S(1)} %get-tuple-element.5), channel_id=1, replica_groups=mesh['member'=8,'band'=4] {'band'}, dimensions={0} | all-to-all | bytes 4718592 | tf_op jit(solution)/shard_map/all_to_all | solution.py:32
  69.1 4.5 all-to-all-start.2
  73.6 0.0 all-gather.5.cloned.1.call-start
  73.6 0.7 all-gather.5.cloned.1.call-update
  74.3 42.2 %all-to-all-done.2 = f32[4,192,768]{2,1,0:T(8,128)} async-done(((f32[4,192,768]{2,1,0:T(8,128)}), f32[4,192,768]{2,1,0:T(8,128)}, u32[]{:S(2)}, u32[]{:S(2)}) %all-to-all-start.2) | async-done | bytes 2359328 | tf_op jit(solution)/shard_map/all_to_all | solution.py:32
  116.6 4.5 all-to-all-start.4
  121.1 28.7 %all-to-all-done.4 = f32[4,192,768]{2,1,0:T(8,128)} async-done(((f32[4,192,768]{2,1,0:T(8,128)}), f32[4,192,768]{2,1,0:T(8,128)}, u32[]{:S(2)}, u32[]{:S(2)}) %all-to-all-start.4) | async-done | bytes 2359328 | tf_op jit(solution)/shard_map/all_to_all | solution.py:32
  149.9 4.5 all-to-all-start.6
  154.4 17.8 %fusion.28 = f32[1024,768]{1,0:T(8,128)} fusion(f32[768,768]{1,0:T(8,128)S(1)} %bitcast.20, s32[768]{0:T(1024)S(1)} %add_select_fusion.1, pred[768]{0:T(1024)(128)(4,1)S(1)} %iota_compare_fusion), kind=kOutput, calls=%fused_computation.45 | convolution fusion | flops 3636461568 | bytes 5508864 | tf_op jit(solution)/shard_map/xa,ab->xb/dot_general | solution.py:40
  172.2 19.6 %fusion.25 = f32[1024,768]{1,0:T(8,128)} fusion(f32[768,768]{1,0:T(8,128)} %bitcast.2, s32[768]{0:T(1024)S(1)} %add_select_fusion.1, pred[768]{0:T(1024)(128)(4,1)S(1)} %iota_compare_fusion), kind=kOutput, calls=%fused_computation.42 | convolution fusion | flops 3636461568 | bytes 5508864 | tf_op jit(solution)/shard_map/xa,ab->xb/dot_general | solution.py:40
  191.7 19.8 %fusion.22 = f32[1024,768]{1,0:T(8,128)} fusion(f32[768,768]{1,0:T(8,128)} %bitcast.4, s32[768]{0:T(1024)S(1)} %add_select_fusion.1, pred[768]{0:T(1024)(128)(4,1)S(1)} %iota_compare_fusion), kind=kOutput, calls=%fused_computation.39 | convolution fusion | flops 3636461568 | bytes 5508864 | tf_op jit(solution)/shard_map/xa,ab->xb/dot_general | solution.py:40
  211.5 0.0 all-to-all-done.6
  211.5 19.5 %fusion.19 = f32[1024,768]{1,0:T(8,128)} fusion(f32[768,768]{1,0:T(8,128)} %bitcast.6, s32[768]{0:T(1024)S(1)} %add_select_fusion.1, pred[768]{0:T(1024)(128)(4,1)S(1)} %iota_compare_fusion), kind=kOutput, calls=%fused_computation.36 | convolution fusion | flops 3636461568 | bytes 5508864 | tf_op jit(solution)/shard_map/xa,ab->xb/dot_general | solution.py:40
  231.1 0.0 all-gather.3.cloned.1.call-done
  231.1 22.2 %multiply_reduce_fusion.3 = (f32[]{:T(128)}, f32[1024,1024]{1,0:T(8,128)}) fusion(f32[1024,1024]{1,0:T(8,128)} %all-gather.3.cloned.1.call-done, f32[1024,768]{1,0:T(8,128)} %fusion.28, s32[768]{0:T(1024)S(1)} %add_select_fusion.1, pred[768]{0:T(1024)(128)(4,1)S(1)} %iota_compare_fusion), kind=kOutput, calls=%fused_computation.19 | convolution fusion | flops 4847566848 | bytes 11538180 | tf_op jit(solution)/shard_map/yb,xb->yx/dot_general | solution.py:41
  254.0 0.0 all-gather.5.cloned.1.call-done
  254.1 26.3 %fusion = f32[768,1024]{1,0:T(8,128)S(1)} fusion(f32[1024,1024]{1,0:T(8,128)} %all-gather.5.cloned.1.call-done, f32[1024,1024]{1,0:T(8,128)} %get-tuple-element.16, f32[]{:T(128)S(6)} %sqrt.12, f32[768]{0:T(1024)S(1)} %select_multiply_fusion, s32[768]{0:T(1024)S(1)} %add_select_fusion.1, pred[768]{0:T(1024)(128)(4,1)S(1)} %iota_compare_fusion), kind=kOutput, calls=%fused_computation.8 | convolution fusion | flops 4848615424 | bytes 11541252 | tf_op jit(solution)/shard_map/ax,yx->ay/dot_general | solution.py:46
  280.4 17.9 %fusion.39 = f32[768,768]{1,0:T(8,128)} fusion(f32[768,1024]{1,0:T(8,128)S(1)} %fusion, f32[768]{0:T(1024)S(1)} %select_multiply_fusion, s32[768]{0:T(1024)S(1)} %add_select_fusion.1, pred[768]{0:T(1024)(128)(4,1)S(1)} %iota_compare_fusion), kind=kOutput, calls=%fused_computation.56 | convolution fusion | flops 3636461568 | bytes 5511936 | tf_op jit(solution)/shard_map/ay,by->ab/dot_general | solution.py:47
  298.3 3.6 all-to-all-start.1
  301.9 22.2 %multiply_reduce_fusion.2 = (f32[]{:T(128)}, f32[1024,1024]{1,0:T(8,128)}) fusion(f32[1024,1024]{1,0:T(8,128)} %all-gather.3.cloned.1.call-done, f32[1024,768]{1,0:T(8,128)} %fusion.25, s32[768]{0:T(1024)S(1)} %add_select_fusion.1, pred[768]{0:T(1024)(128)(4,1)S(1)} %iota_compare_fusion), kind=kOutput, calls=%fused_computation.17 | convolution fusion | flops 4847566848 | bytes 11538180 | tf_op jit(solution)/shard_map/yb,xb->yx/dot_general | solution.py:41
  324.9 26.2 %fusion.1 = f32[768,1024]{1,0:T(8,128)S(1)} fusion(f32[1024,1024]{1,0:T(8,128)} %all-gather.5.cloned.1.call-done, f32[1024,1024]{1,0:T(8,128)} %get-tuple-element.14, f32[]{:T(128)S(6)} %sqrt.13, f32[768]{0:T(1024)S(1)} %select_multiply_fusion, s32[768]{0:T(1024)S(1)} %add_select_fusion.1, pred[768]{0:T(1024)(128)(4,1)S(1)} %iota_compare_fusion), kind=kOutput, calls=%fused_computation.9 | convolution fusion | flops 4848615424 | bytes 11541252 | tf_op jit(solution)/shard_map/ax,yx->ay/dot_general | solution.py:46
  351.1 17.8 %fusion.36 = f32[768,768]{1,0:T(8,128)} fusion(f32[768,1024]{1,0:T(8,128)S(1)} %fusion.1, f32[768]{0:T(1024)S(1)} %select_multiply_fusion, s32[768]{0:T(1024)S(1)} %add_select_fusion.1, pred[768]{0:T(1024)(128)(4,1)S(1)} %iota_compare_fusion), kind=kOutput, calls=%fused_computation.53 | convolution fusion | flops 3636461568 | bytes 5511936 | tf_op jit(solution)/shard_map/ay,by->ab/dot_general | solution.py:47
  368.9 0.0 all-to-all-done.1
  368.9 4.5 all-to-all-start.3
  373.4 22.2 %multiply_reduce_fusion.1 = (f32[]{:T(128)}, f32[1024,1024]{1,0:T(8,128)}) fusion(f32[1024,1024]{1,0:T(8,128)} %all-gather.3.cloned.1.call-done, f32[1024,768]{1,0:T(8,128)} %fusion.22, s32[768]{0:T(1024)S(1)} %add_select_fusion.1, pred[768]{0:T(1024)(128)(4,1)S(1)} %iota_compare_fusion), kind=kOutput, calls=%fused_computation.15 | convolution fusion | flops 4847566848 | bytes 11538180 | tf_op jit(solution)/shard_map/yb,xb->yx/dot_general | solution.py:41
  396.4 26.5 %fusion.2 = f32[768,1024]{1,0:T(8,128)S(1)} fusion(f32[1024,1024]{1,0:T(8,128)} %all-gather.5.cloned.1.call-done, f32[1024,1024]{1,0:T(8,128)} %get-tuple-element.12, f32[]{:T(128)S(6)} %sqrt.14, f32[768]{0:T(1024)S(1)} %select_multiply_fusion, s32[768]{0:T(1024)S(1)} %add_select_fusion.1, pred[768]{0:T(1024)(128)(4,1)S(1)} %iota_compare_fusion), kind=kOutput, calls=%fused_computation.10 | convolution fusion | flops 4848615424 | bytes 11541252 | tf_op jit(solution)/shard_map/ax,yx->ay/dot_general | solution.py:46
  422.9 17.7 %fusion.33 = f32[768,768]{1,0:T(8,128)} fusion(f32[768,1024]{1,0:T(8,128)S(1)} %fusion.2, f32[768]{0:T(1024)S(1)} %select_multiply_fusion, s32[768]{0:T(1024)S(1)} %add_select_fusion.1, pred[768]{0:T(1024)(128)(4,1)S(1)} %iota_compare_fusion), kind=kOutput, calls=%fused_computation.50 | convolution fusion | flops 3636461568 | bytes 5511936 | tf_op jit(solution)/shard_map/ay,by->ab/dot_general | solution.py:47
  440.5 0.0 all-to-all-done.3
  440.5 4.5 all-to-all-start.5
  445.0 22.2 %multiply_reduce_fusion = (f32[]{:T(128)}, f32[1024,1024]{1,0:T(8,128)}) fusion(f32[1024,1024]{1,0:T(8,128)} %all-gather.3.cloned.1.call-done, f32[1024,768]{1,0:T(8,128)} %fusion.19, s32[768]{0:T(1024)S(1)} %add_select_fusion.1, pred[768]{0:T(1024)(128)(4,1)S(1)} %iota_compare_fusion), kind=kOutput, calls=%fused_computation.13 | convolution fusion | flops 4847566848 | bytes 11538180 | tf_op jit(solution)/shard_map/yb,xb->yx/dot_general | solution.py:41
  467.9 26.3 %fusion.3 = f32[768,1024]{1,0:T(8,128)S(1)} fusion(f32[1024,1024]{1,0:T(8,128)} %all-gather.5.cloned.1.call-done, f32[1024,1024]{1,0:T(8,128)} %get-tuple-element.10, f32[]{:T(128)S(6)} %sqrt.15, f32[768]{0:T(1024)S(1)} %select_multiply_fusion, s32[768]{0:T(1024)S(1)} %add_select_fusion.1, pred[768]{0:T(1024)(128)(4,1)S(1)} %iota_compare_fusion), kind=kOutput, calls=%fused_computation.11 | convolution fusion | flops 4848615424 | bytes 11541252 | tf_op jit(solution)/shard_map/ax,yx->ay/dot_general | solution.py:46
  494.2 17.7 %fusion.30 = f32[768,768]{1,0:T(8,128)} fusion(f32[768,1024]{1,0:T(8,128)S(1)} %fusion.3, f32[768]{0:T(1024)S(1)} %select_multiply_fusion, s32[768]{0:T(1024)S(1)} %add_select_fusion.1, pred[768]{0:T(1024)(128)(4,1)S(1)} %iota_compare_fusion), kind=kOutput, calls=%fused_computation.47 | convolution fusion | flops 3636461568 | bytes 5511936 | tf_op jit(solution)/shard_map/ay,by->ab/dot_general | solution.py:47
  511.9 0.0 all-to-all-done.5
  511.9 32.1 %all_to_all.41 = f32[4,192,768]{2,1,0:T(8,128)S(1)} all-to-all(f32[4,192,768]{2,1,0:T(8,128)} %bitcast.24), channel_id=1, replica_groups=mesh['member'=8,'band'=4] {'band'}, dimensions={0} | all-to-all | bytes 4718592 | tf_op jit(solution)/shard_map/all_to_all | solution.py:49
  544.0 6.2 %pad_maximum_fusion = f32[16,192,768]{2,1,0:T(8,128)} fusion(f32[4,192,768]{2,1,0:T(8,128)S(1)} %all_to_all.41, f32[4,192,768]{2,1,0:T(8,128)} %all-to-all-done.5, f32[4,192,768]{2,1,0:T(8,128)} %all-to-all-done.3, f32[4,192,768]{2,1,0:T(8,128)S(1)} %all-to-all-done.1), kind=kLoop, calls=%fused_computation | loop fusion | flops 7077888 | bytes 18874368 | tf_op jit(solution)/shard_map/concatenate | solution.py:50
  (3 shorter events, 0.0 us)
Async XLA Ops:
  6.5 224.5 %all-gather.3.cloned.1.call-start = ((), (), s32[]{:S(2)}) async-start(), calls=%async_computation.8 | async-start | bytes 5242880 | tf_op jit(solution)/shard_map/all_gather | solution.py:35
  69.1 47.5 %all-to-all-start.2 = ((f32[4,192,768]{2,1,0:T(8,128)}), f32[4,192,768]{2,1,0:T(8,128)}, u32[]{:S(2)}, u32[]{:S(2)}) async-start(f32[4,192,768]{2,1,0:T(8,128)} %get-tuple-element.6), calls=%async_computation.2 | async-start | bytes 4718592 | tf_op jit(solution)/shard_map/all_to_all | solution.py:32
  73.6 180.5 %all-gather.5.cloned.1.call-start = ((), (), s32[]{:S(2)}) async-start(), calls=%async_computation.9 | async-start | bytes 5242880 | tf_op jit(solution)/shard_map/all_gather | solution.py:36
  116.6 33.3 %all-to-all-start.4 = ((f32[4,192,768]{2,1,0:T(8,128)}), f32[4,192,768]{2,1,0:T(8,128)}, u32[]{:S(2)}, u32[]{:S(2)}) async-start(f32[4,192,768]{2,1,0:T(8,128)} %get-tuple-element.8), calls=%async_computation.4 | async-start | bytes 4718592 | tf_op jit(solution)/shard_map/all_to_all | solution.py:32
  149.9 61.6 %all-to-all-start.6 = ((f32[4,192,768]{2,1,0:T(8,128)}), f32[4,192,768]{2,1,0:T(8,128)}, u32[]{:S(2)}, u32[]{:S(2)}) async-start(f32[4,192,768]{2,1,0:T(8,128)} %get-tuple-element.7), calls=%async_computation.6 | async-start | bytes 4718592 | tf_op jit(solution)/shard_map/all_to_all | solution.py:32
  298.3 70.6 %all-to-all-start.1 = ((f32[4,192,768]{2,1,0:T(8,128)}), f32[4,192,768]{2,1,0:T(8,128)S(1)}, u32[]{:S(2)}, u32[]{:S(2)}) async-start(f32[4,192,768]{2,1,0:T(8,128)} %bitcast.23), calls=%async_computation.1 | async-start | bytes 4718592 | tf_op jit(solution)/shard_map/all_to_all | solution.py:49
  368.9 71.6 %all-to-all-start.3 = ((f32[4,192,768]{2,1,0:T(8,128)}), f32[4,192,768]{2,1,0:T(8,128)}, u32[]{:S(2)}, u32[]{:S(2)}) async-start(f32[4,192,768]{2,1,0:T(8,128)} %bitcast.22), calls=%async_computation.3 | async-start | bytes 4718592 | tf_op jit(solution)/shard_map/all_to_all | solution.py:49
  440.5 71.4 %all-to-all-start.5 = ((f32[4,192,768]{2,1,0:T(8,128)}), f32[4,192,768]{2,1,0:T(8,128)}, u32[]{:S(2)}, u32[]{:S(2)}) async-start(f32[4,192,768]{2,1,0:T(8,128)} %bitcast.21), calls=%async_computation.5 | async-start | bytes 4718592 | tf_op jit(solution)/shard_map/all_to_all | solution.py:49
Sparse Core Ops, SparseCore 0:
  8.9 59.7 all-gather.2
  76.0 50.1 all-gather.4
where the time goes:
time: 566 us; the launch traced here: 557 us
  matrix products  342 us (60%)
  blocking collectives  87 us (15%)
  waiting for transfers between devices  72.4 us (13%)
  starting transfers between devices  26.2 us (5%)
  between operations  16.8 us (3%)
  local copies, waits for them, and re-layouts  6.85 us (1%)
  other arithmetic  6.19 us (1%)
    dot_general x4, matrix products, on_device(): back = jnp.einsum('ax,yx->ay', analysis, tendency, precision=high)  105 us
    dot_general x4, matrix products, on_device(): grid = jnp.einsum('yb,xb->yx', synthesis, section, precision=high)  88.9 us
    dot_general x4, matrix products, on_device(): section = jnp.einsum('xa,ab->xb', synthesis, field, precision=high)  76.7 us
    dot_general x4, matrix products, on_device(): done = jnp.einsum('ay,by->ab', back, analysis, precision=high)  71 us
    all_to_all x3, waiting for transfers between devices, on_device(): lax.all_to_all(spectral[at:at + ways], 'band', split_axis=0, concat_axis=...  71 us
    all_to_all x1, blocking collectives, on_device(): lax.all_to_all(spectral[at:at + ways], 'band', split_axis=0, concat_axis=...  55 us
    all_to_all x1, blocking collectives, on_device(): lax.all_to_all(done, 'band', split_axis=0, concat_axis=0, tiled=True)  32.1 us
    all_to_all x3, starting transfers between devices, on_device(): lax.all_to_all(spectral[at:at + ways], 'band', split_axis=0, concat_axis=...  13.5 us
  transfers between devices with their start and end apart: 8, of which 2 were waited for; matrix products, arithmetic and copies ran while one was open for 55% of the time, Pallas kernels for 0%

commit v1 on v0

v1 whole, which is shorter than its diff:
```python
import functools
import math

import jax
import jax.numpy as jnp
import numpy as np
from jax import lax
from jax.experimental import pallas as pl
from jax.experimental.pallas import tpu as pltpu
from jax.sharding import PartitionSpec as P

MESH = pl.DeviceIdType.MESH
F32 = jnp.float32
BF16 = jnp.bfloat16
LANES = 128
ROWS = 32
TILE = 256


def seeds(cells, coeffs):
    half = coeffs // 2
    wave = np.arange(half)

    def pair(points, transposed):
        turns = np.outer(points, wave) % cells
        angles = turns * (2.0 * math.pi / cells)
        both = np.stack([np.cos(angles), np.sin(angles)])
        return np.swapaxes(both, 1, 2).astype(np.float32) if transposed else both.astype(np.float32)

    return (
        pair(np.arange(0, cells, ROWS), False),
        pair(np.arange(ROWS), False),
        pair(np.arange(0, cells, LANES), True),
        pair(np.arange(LANES), True),
    )


def split(value):
    high = value.astype(BF16)
    return high, (value - high.astype(F32)).astype(BF16)


def dot3(a_high, a_low, b_high, b_low):
    dot = functools.partial(jnp.dot, preferred_element_type=F32)
    return dot(a_high, b_high) + dot(a_low, b_high) + dot(a_high, b_low)


def round_trip(
    ways, spectral, coupling, quadratic, coarse_r, fine_r, coarse_l, fine_l, out,
    fields, natural, turned, basis_h, basis_l, basis_th, basis_tl,
    field_h, field_l, half_h, half_l, product, tend_h, tend_l, back_h, back_l, total, result,
    fs, fr, fo, cs, cr, co, rs, bs, br, bo,
):
    levels, band, coeffs = spectral.shape
    rows, cells = coupling.shape
    half = coeffs // 2
    groups = levels // ways
    cores = 2 if ways % 2 == 0 else 1
    chips = ways // cores
    me = lax.axis_index("band")
    chip, core = me // cores, me % cores

    def partner(away, side):
        return ((chip + away) % chips) * cores + (core + side) % cores

    def band_of(index):
        return pl.ds(pl.multiple_of(index * band, band), band)

    def rows_of(index):
        return pl.ds(pl.multiple_of(index * rows, rows), rows)

    def send_field(group, to):
        return pltpu.make_async_remote_copy(
            src_ref=spectral.at[group * ways + to],
            dst_ref=fields.at[group, band_of(me)],
            send_sem=fs.at[group, to],
            recv_sem=fr.at[group, me],
            device_id={"band": to},
            device_id_type=MESH,
        )

    def take_field(group, source):
        return pltpu.make_async_remote_copy(
            src_ref=spectral.at[group * ways + me],
            dst_ref=fields.at[group, band_of(source)],
            send_sem=fs.at[group, source],
            recv_sem=fr.at[group, source],
            device_id={"band": source},
            device_id_type=MESH,
        )

    def own_field(group):
        return pltpu.make_async_copy(
            spectral.at[group * ways + me], fields.at[group, band_of(me)], fo.at[group]
        )

    weights = (coupling, quadratic)

    def send_weight(which, to):
        return pltpu.make_async_remote_copy(
            src_ref=weights[which],
            dst_ref=natural.at[which, rows_of(me)],
            send_sem=cs.at[which, to],
            recv_sem=cr.at[which, me],
            device_id={"band": to},
            device_id_type=MESH,
        )

    def take_weight(which, source):
        return pltpu.make_async_remote_copy(
            src_ref=weights[which],
            dst_ref=natural.at[which, rows_of(source)],
            send_sem=cs.at[which, source],
            recv_sem=cr.at[which, source],
            device_id={"band": source},
            device_id_type=MESH,
        )

    def relay_weight(which, source, to):
        return pltpu.make_async_remote_copy(
            src_ref=natural.at[which, rows_of(source)],
            dst_ref=natural.at[which, rows_of(source)],
            send_sem=rs.at[which, source],
            recv_sem=cr.at[which, source],
            device_id={"band": to},
            device_id_type=MESH,
        )

    def own_weight(which):
        return pltpu.make_async_copy(weights[which], natural.at[which, rows_of(me)], co.at[which])

    def send_result(group, to):
        return pltpu.make_async_remote_copy(
            src_ref=result.at[group, band_of(to)],
            dst_ref=out.at[group * ways + me],
            send_sem=bs.at[group, to],
            recv_sem=br.at[group, me],
            device_id={"band": to},
            device_id_type=MESH,
        )

    def take_result(group, source):
        return pltpu.make_async_remote_copy(
            src_ref=result.at[group, band_of(source)],
            dst_ref=out.at[group * ways + source],
            send_sem=bs.at[group, source],
            recv_sem=br.at[group, source],
            device_id={"band": source},
            device_id_type=MESH,
        )

    def own_result(group):
        return pltpu.make_async_copy(
            result.at[group, band_of(me)], out.at[group * ways + me], bo.at[group]
        )

    def step_partner(step):
        return partner((step // cores + 1) % chips, cores - 1 - step % cores)

    barrier = pltpu.get_barrier_semaphore()
    for step in range(ways - 1):
        pl.semaphore_signal(barrier, inc=1, device_id={"band": step_partner(step)}, device_id_type=MESH)
    pl.semaphore_wait(barrier, ways - 1)

    def start_fields(group):
        for step in range(ways - 1):
            send_field(group, step_partner(step)).start()
        own_field(group).start()

    start_fields(0)
    for which in range(2):
        for away in range(1, chips):
            send_weight(which, partner(away, 0)).start()
        for side in range(1, cores):
            send_weight(which, partner(0, side)).start()
        own_weight(which).start()
    for group in range(1, groups):
        start_fields(group)

    def rows_table(block, _):
        one, at = pl.ds(block, 1), pl.ds(pl.multiple_of(block * ROWS, ROWS), ROWS)
        cos_u, sin_u = coarse_r[0, one, :], coarse_r[1, one, :]
        cos_v, sin_v = fine_r[0], fine_r[1]
        high, low = split(cos_u * cos_v - sin_u * sin_v)
        basis_h[at, :half], basis_l[at, :half] = high, low
        high, low = split(sin_u * cos_v + cos_u * sin_v)
        basis_h[at, half:], basis_l[at, half:] = high, low
        return _

    lax.fori_loop(0, cells // ROWS, rows_table, 0)
    chunk = half // 6 if half % 96 == 0 else half

    def lanes_table(block, _):
        at = pl.ds(pl.multiple_of(block * chunk, chunk), chunk)
        below = pl.ds(pl.multiple_of(half + block * chunk, chunk), chunk)
        cos_v, sin_v = fine_l[0, at, :], fine_l[1, at, :]
        cos_w, sin_w = coarse_l[0, at, :], coarse_l[1, at, :]
        for word in range(cells // LANES):
            lanes = slice(word * LANES, (word + 1) * LANES)
            cos_u, sin_u = cos_w[:, word : word + 1], sin_w[:, word : word + 1]
            high, low = split(cos_u * cos_v - sin_u * sin_v)
            basis_th[at, lanes], basis_tl[at, lanes] = high, low
            high, low = split(sin_u * cos_v + cos_u * sin_v)
            basis_th[below, lanes], basis_tl[below, lanes] = high, low
        return _

    lax.fori_loop(0, half // chunk, lanes_table, 0)

    def factor(index):
        wave = jnp.where(index < half, index, index - half)
        return jnp.where(wave == 0, 1.0, 2.0) / cells

    def tile(index):
        return pl.ds(pl.multiple_of(index * TILE, TILE), TILE)

    def one_level(group, first):
        for step in range(ways - 1):
            take_field(group, step_partner(step)).wait_recv()
        own_field(group).wait()

        def split_field(index, _):
            at = band_of(index)
            field_h[at, :], field_l[at, :] = split(fields[group, at, :])
            return _

        lax.fori_loop(0, ways, split_field, 0)

        def synth_x(index, _):
            at = tile(index)
            value = dot3(basis_h[at, :], basis_l[at, :], field_h[...], field_l[...])
            half_h[at, :], half_l[at, :] = split(value)
            return _

        lax.fori_loop(0, cells // TILE, synth_x, 0)

        if first:
            for which in range(2):
                for away in range(1, chips):
                    take_weight(which, partner(away, 0)).wait_recv()
                    for side in range(1, cores):
                        relay_weight(which, partner(away, 0), partner(0, side)).start()
                for side in range(1, cores):
                    take_weight(which, partner(0, side)).wait_recv()
                own_weight(which).wait()
            for which in range(2):
                for away in range(1, chips):
                    for side in range(1, cores):
                        take_weight(which, partner(away, side)).wait_recv()

                def turn(index, _):
                    at = pl.ds(pl.multiple_of(index * LANES, LANES), LANES)
                    value = natural[which, at, :].T
                    turned[which, :, at] = value * (1.0 / half) if which == 0 else value
                    return _

                lax.fori_loop(0, cells // LANES, turn, 0)

        total[...] = jnp.zeros_like(total)

        def synth_y(index, _):
            at = tile(index)
            value = dot3(half_h[at, :], half_l[at, :], basis_th[...], basis_tl[...])
            value = value * turned[0, at, :]
            product[at, :] = value
            total[...] += jnp.sum((value * value).reshape(TILE // 8, 8, cells), axis=0)
            return _

        lax.fori_loop(0, cells // TILE, synth_y, 0)
        energy = jnp.sum(jnp.sum(total[...], axis=0, keepdims=True), axis=1, keepdims=True)
        scale = 1.0 / jnp.sqrt(energy * (1.0 / (cells * cells)) + 1e-06)

        def nonlinear(index, _):
            at = tile(index)
            scaled = product[at, :] * scale
            tend_h[at, :], tend_l[at, :] = split(scaled + turned[1, at, :] * scaled * scaled)
            return _

        lax.fori_loop(0, cells // TILE, nonlinear, 0)

        def analyse_x(index, _):
            at = tile(index)
            value = dot3(basis_th[at, :], basis_tl[at, :], tend_h[...], tend_l[...])
            back_h[at, :], back_l[at, :] = split(value)
            return _

        lax.fori_loop(0, coeffs // TILE, analyse_x, 0)
        columns = factor(lax.broadcasted_iota(jnp.int32, (1, coeffs), 1)) * half

        def analyse_y(step, _):
            to = step_partner(step)
            at = band_of(to)
            value = dot3(back_h[at, :], back_l[at, :], basis_h[...], basis_l[...])
            line = factor(lax.broadcasted_iota(jnp.int32, (band, 1), 0) + to * band)
            result[group, at, :] = value * (line * columns)

            @pl.when(step > 0)
            def _send():
                send_result(group, step_partner(step - 1)).start()

            return _

        lax.fori_loop(0, ways, analyse_y, 0)
        own_result(group).start()

    one_level(0, True)
    if groups > 1:

        def later(group, _):
            one_level(group, False)
            return _

        lax.fori_loop(1, groups, later, 0)

    def finish(group, _):
        for step in range(ways - 1):
            other = step_partner(step)
            send_field(group, other).wait_send()
            send_result(group, other).wait_send()
            take_result(group, other).wait_recv()
        own_result(group).wait()
        return _

    for which in range(2):
        for away in range(1, chips):
            send_weight(which, partner(away, 0)).wait_send()
            for side in range(1, cores):
                relay_weight(which, partner(away, 0), partner(0, side)).wait_send()
        for side in range(1, cores):
            send_weight(which, partner(0, side)).wait_send()
    lax.fori_loop(0, groups, finish, 0)


def on_device(spectral, coupling, quadratic):
    levels, band, coeffs = spectral.shape
    rows, cells = coupling.shape
    ways = lax.axis_size("band")
    groups = levels // ways
    anywhere = pl.BlockSpec(memory_space=pl.ANY)
    inside = pl.BlockSpec(memory_space=pltpu.VMEM)
    copies = pltpu.SemaphoreType.DMA
    return pl.pallas_call(
        functools.partial(round_trip, ways),
        out_shape=jax.ShapeDtypeStruct((levels, band, coeffs), F32),
        in_specs=[anywhere] * 3 + [inside] * 4,
        out_specs=anywhere,
        scratch_shapes=[
            pltpu.VMEM((groups, coeffs, coeffs), F32),
            pltpu.VMEM((2, cells, cells), F32),
            pltpu.VMEM((2, cells, cells), F32),
            pltpu.VMEM((cells, coeffs), BF16),
            pltpu.VMEM((cells, coeffs), BF16),
            pltpu.VMEM((coeffs, cells), BF16),
            pltpu.VMEM((coeffs, cells), BF16),
            pltpu.VMEM((coeffs, coeffs), BF16),
            pltpu.VMEM((coeffs, coeffs), BF16),
            pltpu.VMEM((cells, coeffs), BF16),
            pltpu.VMEM((cells, coeffs), BF16),
            pltpu.VMEM((cells, cells), F32),
            pltpu.VMEM((cells, cells), BF16),
            pltpu.VMEM((cells, cells), BF16),
            pltpu.VMEM((coeffs, cells), BF16),
            pltpu.VMEM((coeffs, cells), BF16),
            pltpu.VMEM((8, cells), F32),
            pltpu.VMEM((groups, coeffs, coeffs), F32),
            copies((groups, ways)),
            copies((groups, ways)),
            copies((groups,)),
            copies((2, ways)),
            copies((2, ways)),
            copies((2,)),
            copies((2, ways)),
            copies((groups, ways)),
            copies((groups, ways)),
            copies((groups,)),
        ],
        compiler_params=pltpu.CompilerParams(
            collective_id=0, has_side_effects=True, vmem_limit_bytes=67043328
        ),
        name="round_trip",
    )(spectral, coupling, quadratic, *seeds(cells, coeffs))


def solution(mesh):
    placed = (P("member", "band", None), P(("member", "band"), None), P(("member", "band"), None))
    return jax.shard_map(
        on_device, mesh=mesh, in_specs=placed, out_specs=P("member", "band", None), check_vma=False
    )
```

time: 566 us -> 262 us (0.46); the launches traced: 557 us -> 262 us
  matrix products: 342 us -> 0 us
  Pallas kernels: 0 us -> 254 us
  blocking collectives: 87 us -> 0 us
  waiting for transfers between devices: 72.4 us -> 0 us
  starting transfers between devices: 26.2 us -> 0 us
  between operations: 16.8 us -> 0.01 us
  other arithmetic: 6.19 us -> 0 us
    dot_general x16 -> x0, matrix products: 342 us -> none  [the longest x4 105 us: on_device(): back = jnp.einsum('ax,yx->ay', analysis, tendency, precision=high)]
    pallas_call x0 -> x1, Pallas kernels: none -> 254 us  [on_device(): pl.pallas_call(functools.partial(round_trip, ways), out_shape=jax.ShapeDt...]
    all_to_all x2 -> x0, blocking collectives: 87 us -> none  [the longest x1 55 us: on_device(): lax.all_to_all(spectral[at:at + ways], 'band', split_axis=0, concat_axis=...]
    all_to_all x6 -> x0, waiting for transfers between devices: 71 us -> none  [the longest x3 71 us: on_device(): lax.all_to_all(spectral[at:at + ways], 'band', split_axis=0, concat_axis=...]
    all_to_all x6 -> x0, starting transfers between devices: 26.2 us -> none  [the longest x3 13.5 us: on_device(): lax.all_to_all(spectral[at:at + ways], 'band', split_axis=0, concat_axis=...]
    unnamed x0 -> x1, local copies, waits for them, and re-layouts: none -> 8.26 us
    slice x1 -> x0, local copies, waits for them, and re-layouts: 6.85 us -> none  [on_device(): spectral[at:at + ways]]
    concatenate x1 -> x0, other arithmetic: 6.17 us -> none  [on_device(): return jnp.concatenate(outputs, axis=0)]
  transfers between devices with their start and end apart: 8 -> 0, of which waited for: 2 -> 0; matrix products, arithmetic and copies ran while one was open for 55% -> 0% of each run, Pallas kernels for 0% -> 0%
where the time goes in v1:
time: 262 us
  Pallas kernels  254 us (97%)
  local copies, waits for them, and re-layouts  8.26 us (3%)
    pallas_call x1, Pallas kernels, on_device(): pl.pallas_call(functools.partial(round_trip, ways), out_shape=jax.ShapeDt...  254 us
    unnamed x1, local copies, waits for them, and re-layouts  8.26 us

profile of v1, /device:TPU:0, one launch (start us, length us, event | category | flops | bytes accessed | tf_op | source)
XLA Modules:
  0.0 262.2 jit_solution(14073283402873782724)
XLA Ops:
  0.0 253.9 %round_trip.1 = f32[16,192,768]{2,1,0:T(8,128)} custom-call(f32[16,192,768]{2,1,0:T(8,128)} %spectral.1, f32[256,1024]{1,0:T(8,128)} %coupling.1, f32[256,1024]{1,0:T(8,128)} %quadratic.1, f32[2,32,384]{2,1,0:T(8,128)} %constant.8.clone.coarse_r, f32[2,32,384]{2,1,0:T(8,128)} %constant.9.clone.fine_r, f32[2,384,8]{2,1,0:T(8,128)} %constant.10.clone.coarse_l, ...), custom_call_target="tpu_custom_call" | custom-call | tf_op jit(solution)/shard_map/round_trip/pallas_call | solution.py:341
  253.9 8.3 %copy.9 = f32[16,192,768]{2,1,0:T(8,128)} copy(f32[16,192,768]{2,1,0:T(8,128)} %round_trip.1) | data formatting | bytes 18874368

commit v2 on v1

--- a/solution.py
+++ b/solution.py
@@ -46,10 +46,10 @@
 
 
 def round_trip(
-    ways, spectral, coupling, quadratic, coarse_r, fine_r, coarse_l, fine_l, out,
-    fields, natural, turned, basis_h, basis_l, basis_th, basis_tl,
-    field_h, field_l, half_h, half_l, product, tend_h, tend_l, back_h, back_l, total, result,
-    fs, fr, fo, cs, cr, co, rs, bs, br, bo,
+    ways, spectral, coupling, quadratic, seed_cr, seed_fr, seed_cl, seed_fl, out,
+    coarse_r, fine_r, coarse_l, fine_l, fields, natural, turned, basis_h, basis_l, basis_th, basis_tl,
+    field_h, field_l, half_h, half_l, tend_h, tend_l, back_h, back_l, total,
+    ss, fs, fr, fo, cs, cr, co, rs, bs, br, bo,
 ):
     levels, band, coeffs = spectral.shape
     rows, cells = coupling.shape
@@ -131,7 +131,7 @@
 
     def send_result(group, to):
         return pltpu.make_async_remote_copy(
-            src_ref=result.at[group, band_of(to)],
+            src_ref=fields.at[group, band_of(to)],
             dst_ref=out.at[group * ways + me],
             send_sem=bs.at[group, to],
             recv_sem=br.at[group, me],
@@ -141,7 +141,7 @@
 
     def take_result(group, source):
         return pltpu.make_async_remote_copy(
-            src_ref=result.at[group, band_of(source)],
+            src_ref=fields.at[group, band_of(source)],
             dst_ref=out.at[group * ways + source],
             send_sem=bs.at[group, source],
             recv_sem=br.at[group, source],
@@ -151,7 +151,7 @@
 
     def own_result(group):
         return pltpu.make_async_copy(
-            result.at[group, band_of(me)], out.at[group * ways + me], bo.at[group]
+            fields.at[group, band_of(me)], out.at[group * ways + me], bo.at[group]
         )
 
     def step_partner(step):
@@ -168,6 +168,14 @@
         own_field(group).start()
 
     start_fields(0)
+    seeded = [
+        pltpu.make_async_copy(source, target, ss.at[number])
+        for number, (source, target) in enumerate(
+            ((seed_cr, coarse_r), (seed_fr, fine_r), (seed_cl, coarse_l), (seed_fl, fine_l))
+        )
+    ]
+    for copy in seeded:
+        copy.start()
     for which in range(2):
         for away in range(1, chips):
             send_weight(which, partner(away, 0)).start()
@@ -176,6 +184,9 @@
         own_weight(which).start()
     for group in range(1, groups):
         start_fields(group)
+
+    for copy in seeded:
+        copy.wait()
 
     def rows_table(block, _):
         one, at = pl.ds(block, 1), pl.ds(pl.multiple_of(block * ROWS, ROWS), ROWS)
@@ -246,6 +257,7 @@
                 for away in range(1, chips):
                     for side in range(1, cores):
                         take_weight(which, partner(away, side)).wait_recv()
+                        relay_weight(which, partner(away, 0), partner(0, side)).wait_send()
 
                 def turn(index, _):
                     at = pl.ds(pl.multiple_of(index * LANES, LANES), LANES)
@@ -261,7 +273,7 @@
             at = tile(index)
             value = dot3(half_h[at, :], half_l[at, :], basis_th[...], basis_tl[...])
             value = value * turned[0, at, :]
-            product[at, :] = value
+            natural[0, at, :] = value
             total[...] += jnp.sum((value * value).reshape(TILE // 8, 8, cells), axis=0)
             return _
 
@@ -271,7 +283,7 @@
 
         def nonlinear(index, _):
             at = tile(index)
-            scaled = product[at, :] * scale
+            scaled = natural[0, at, :] * scale
             tend_h[at, :], tend_l[at, :] = split(scaled + turned[1, at, :] * scaled * scaled)
             return _
 
@@ -291,7 +303,7 @@
             at = band_of(to)
             value = dot3(back_h[at, :], back_l[at, :], basis_h[...], basis_l[...])
             line = factor(lax.broadcasted_iota(jnp.int32, (band, 1), 0) + to * band)
-            result[group, at, :] = value * (line * columns)
+            fields[group, at, :] = value * (line * columns)
 
             @pl.when(step > 0)
             def _send():
@@ -323,8 +335,6 @@
     for which in range(2):
         for away in range(1, chips):
             send_weight(which, partner(away, 0)).wait_send()
-            for side in range(1, cores):
-                relay_weight(which, partner(away, 0), partner(0, side)).wait_send()
         for side in range(1, cores):
             send_weight(which, partner(0, side)).wait_send()
     lax.fori_loop(0, groups, finish, 0)
@@ -335,15 +345,17 @@
     rows, cells = coupling.shape
     ways = lax.axis_size("band")
     groups = levels // ways
-    anywhere = pl.BlockSpec(memory_space=pl.ANY)
+    anywhere = pl.BlockSpec(memory_space=pltpu.HBM)
     inside = pl.BlockSpec(memory_space=pltpu.VMEM)
+    tables = seeds(cells, coeffs)
     copies = pltpu.SemaphoreType.DMA
     return pl.pallas_call(
         functools.partial(round_trip, ways),
-        out_shape=jax.ShapeDtypeStruct((levels, band, coeffs), F32),
-        in_specs=[anywhere] * 3 + [inside] * 4,
-        out_specs=anywhere,
+        out_shape=pltpu.VMEM((levels, band, coeffs), F32),
+        in_specs=[anywhere] * 7,
+        out_specs=inside,
         scratch_shapes=[
+            *(pltpu.VMEM(table.shape, F32) for table in tables),
             pltpu.VMEM((groups, coeffs, coeffs), F32),
             pltpu.VMEM((2, cells, cells), F32),
             pltpu.VMEM((2, cells, cells), F32),
@@ -355,13 +367,12 @@
             pltpu.VMEM((coeffs, coeffs), BF16),
             pltpu.VMEM((cells, coeffs), BF16),
             pltpu.VMEM((cells, coeffs), BF16),
-            pltpu.VMEM((cells, cells), F32),
             pltpu.VMEM((cells, cells), BF16),
             pltpu.VMEM((cells, cells), BF16),
             pltpu.VMEM((coeffs, cells), BF16),
             pltpu.VMEM((coeffs, cells), BF16),
             pltpu.VMEM((8, cells), F32),
-            pltpu.VMEM((groups, coeffs, coeffs), F32),
+            copies((len(tables),)),
             copies((groups, ways)),
             copies((groups, ways)),
             copies((groups,)),
@@ -374,10 +385,10 @@
             copies((groups,)),
         ],
         compiler_params=pltpu.CompilerParams(
-            collective_id=0, has_side_effects=True, vmem_limit_bytes=67043328
+            collective_id=0, has_side_effects=True, vmem_limit_bytes=50 * 2**20
         ),
         name="round_trip",
-    )(spectral, coupling, quadratic, *seeds(cells, coeffs))
+    )(spectral, coupling, quadratic, *tables)
 
 
 def solution(mesh):

time: 262 us -> 257 us (0.981)
  local copies, waits for them, and re-layouts: 8.26 us -> 3.74 us
    unnamed x1, local copies, waits for them, and re-layouts: 8.26 us -> 3.74 us
where the time goes in v2:
time: 257 us; the launch traced here: 256 us
  Pallas kernels  253 us (98%)
  local copies, waits for them, and re-layouts  3.74 us (1%)
    pallas_call x1, Pallas kernels, on_device(): pl.pallas_call(functools.partial(round_trip, ways), out_shape=pltpu.VMEM(...  253 us

profile of v2, /device:TPU:0, one launch (start us, length us, event | category | flops | bytes accessed | tf_op | source)
XLA Modules:
  0.0 256.4 jit_solution(2229574223773294932)
XLA Ops:
  0.0 252.6 %round_trip.1 = f32[16,192,768]{2,1,0:T(8,128)S(1)} custom-call(f32[16,192,768]{2,1,0:T(8,128)} %spectral.1, f32[256,1024]{1,0:T(8,128)} %coupling.1, f32[256,1024]{1,0:T(8,128)} %quadratic.1, f32[2,32,384]{2,1,0:T(8,128)} %constant.8.clone.seed_cr, f32[2,32,384]{2,1,0:T(8,128)} %constant.9.clone.seed_fr, f32[2,384,8]{2,1,0:T(8,128)} %constant.10.clone.seed_cl, ...), custom_call_target="tpu_custom_call" | custom-call | tf_op jit(solution)/shard_map/round_trip/pallas_call | solution.py:352
  252.6 3.7 %copy.9 = f32[16,192,768]{2,1,0:T(8,128)} copy(f32[16,192,768]{2,1,0:T(8,128)S(1)} %round_trip.1) | data formatting | bytes 18874368

commit v3 on v2

--- a/solution.py
+++ b/solution.py
@@ -15,6 +15,9 @@
 LANES = 128
 ROWS = 32
 TILE = 256
+PIECES = 4
+SHARED = 2
+EARLY = 1
 
 
 def seeds(cells, coeffs):
@@ -391,8 +394,579 @@
     )(spectral, coupling, quadratic, *tables)
 
 
+def paired(
+    spectral, coupling, quadratic, seed_cr, seed_fr, seed_cl, seed_fl, out, natural,
+    coarse_r, fine_r, coarse_l, fine_l, fields, landed, turned, basis_h, basis_l, basis_th, basis_tl,
+    wide_h, wide_l, side_h, side_l, product, staged, total,
+    ss, fs, fr, fo, gs, ls, lr, ws, kr, cs, cr, co, rs, xs, bs, br, bo,
+):
+    levels, band, coeffs = spectral.shape
+    rows, cells = coupling.shape
+    half = coeffs // 2
+    home, guest = levels * 3 // 8, levels // 8
+    piece = band // PIECES
+    guests = 2 * guest * PIECES
+    tail = pl.ds(SHARED * piece, band - SHARED * piece)
+    member, me = lax.axis_index("member"), lax.axis_index("band")
+    m, x, c = member % 2, me // 2, me % 2
+    near = m == x
+    far = m != x
+    same = 1 - (m - x) * (m - x)
+    weights = (coupling, quadratic)
+
+    def device(row, column, core):
+        return {"member": member - m + row, "band": column * 2 + core}
+
+    def remote(source, target, sent, received, to):
+        return pltpu.make_async_remote_copy(
+            src_ref=source, dst_ref=target, send_sem=sent, recv_sem=received,
+            device_id=to, device_id_type=MESH,
+        )
+
+    def band_of(index):
+        return pl.ds(pl.multiple_of(index * band, band), band)
+
+    def part_of(index, number):
+        return pl.ds(pl.multiple_of(index * band + number * piece, piece), piece)
+
+    def tail_of(index):
+        return pl.ds(pl.multiple_of(index * band + SHARED * piece, piece), band - SHARED * piece)
+
+    def rows_of(index):
+        return pl.ds(pl.multiple_of(index * rows, rows), rows)
+
+    sibling = device(m, x, 1 - c)
+    def near_sibling(slot):
+        return remote(
+            spectral.at[(1 - c) * home + slot], fields.at[slot, band_of(me)],
+            fs.at[slot, 0], fr.at[slot, me], sibling,
+        )
+
+    def near_own(slot):
+        return pltpu.make_async_copy(
+            spectral.at[c * home + slot], fields.at[slot, band_of(me)], fo.at[slot]
+        )
+
+    def near_guest(slot, core):
+        return remote(
+            spectral.at[2 * home + core * guest + slot], fields.at[slot, band_of(me)],
+            gs.at[slot, core], fr.at[slot, me], device(1 - m, x, core),
+        )
+
+    def far_home(slot, core):
+        return remote(
+            spectral.at[core * home + slot], fields.at[slot, band_of(me)],
+            fs.at[slot, core], fr.at[slot, me], device(m, 1 - x, core),
+        )
+
+    def far_tail(core):
+        slot = EARLY
+        return remote(
+            spectral.at[core * home + slot, tail], fields.at[slot, tail_of(me)],
+            fs.at[slot, core], fr.at[slot, me], device(m, 1 - x, core),
+        )
+
+    def far_piece(number):
+        if number < guests:
+            slot, core, part = number // (2 * PIECES), number // PIECES % 2, number % PIECES
+            level = 2 * home + core * guest + slot
+        else:
+            core, part = (number - guests) // SHARED, (number - guests) % SHARED
+            level = core * home + EARLY
+        return remote(
+            spectral.at[level, pl.ds(part * piece, piece)], landed.at[number],
+            ls.at[number], lr.at[number], device(1 - m, x, c),
+        )
+
+    def forward(number, target, to):
+        @pl.when(near)
+        def _forward():
+            far_piece_landed(number).wait_recv()
+            remote(landed.at[number], target, ws.at[number], kr.at[number, c], to).start()
+
+    def far_piece_landed(number):
+        return remote(
+            landed.at[number], landed.at[number], ls.at[number], lr.at[number], device(1 - m, x, c)
+        )
+
+    def forwarded(number):
+        return remote(
+            landed.at[number], landed.at[number], ws.at[number], kr.at[number, c], sibling
+        )
+
+    def forward_guest(number):
+        slot, core, part = number // (2 * PIECES), number // PIECES % 2, number % PIECES
+        forward(number, fields.at[slot, part_of(me, part)], device(m, 1 - x, core))
+
+    def forward_home(index):
+        core, part = index // SHARED, index % SHARED
+        forward(
+            guests + index, fields.at[EARLY, part_of(me, part)], device(1 - m, 1 - x, core)
+        )
+
+    def taken(target, received):
+        return remote(target, target, ss.at[0], received, sibling)
+
+    def take_fields(slot):
+        @pl.when(near)
+        def _home():
+            near_own(slot).wait()
+            other = 2 * x + 1 - c
+            taken(fields.at[slot, band_of(other)], fr.at[slot, other]).wait_recv()
+
+            @pl.when(slot != EARLY)
+            def _whole():
+                for core in range(2):
+                    source = 2 * (1 - x) + core
+                    taken(fields.at[slot, band_of(source)], fr.at[slot, source]).wait_recv()
+
+            @pl.when(slot == EARLY)
+            def _parts():
+                for core in range(2):
+                    source = 2 * (1 - x) + core
+                    taken(fields.at[slot, tail_of(source)], fr.at[slot, source]).wait_recv()
+                    for part in range(SHARED):
+                        number = guests + c * SHARED + part
+                        taken(fields.at[slot, part_of(source, part)], kr.at[number, core]).wait_recv()
+
+        @pl.when(far)
+        def _guest():
+            for core in range(2):
+                source = 2 * x + core
+                taken(fields.at[slot, band_of(source)], fr.at[slot, source]).wait_recv()
+                source = 2 * (1 - x) + core
+                for part in range(PIECES):
+                    number = (slot * 2 + c) * PIECES + part
+                    taken(fields.at[slot, part_of(source, part)], kr.at[number, core]).wait_recv()
+
+    def give(which, number, to):
+        return remote(
+            weights[which], natural.at[which, rows_of(me)], cs.at[which, number], cr.at[which, me], to
+        )
+
+    def weight(which, source):
+        at = natural.at[which, rows_of(source)]
+        return taken(at, cr.at[which, source])
+
+    def relay(which, source, number, to):
+        at = natural.at[which, rows_of(source)]
+        return remote(at, at, rs.at[which, number], cr.at[which, source], to)
+
+    close, remote_band = 2 * x + c, 2 * (1 - x) + c
+
+    def stage(which, column):
+        copy = pltpu.make_async_copy(
+            natural.at[which, pl.ds(pl.multiple_of(column * 2 * rows, 2 * rows), 2 * rows)],
+            staged, xs.at[which, column],
+        )
+        copy.start()
+        copy.wait()
+
+    def gather_close(which):
+        other = 2 * x + 1 - c
+
+        @pl.when(near)
+        def _home():
+            own = pltpu.make_async_copy(weights[which], staged.at[rows_of(c)], co.at[which])
+            own.start()
+            weight(which, other).wait_recv()
+            rest = pltpu.make_async_copy(
+                natural.at[which, rows_of(other)], staged.at[rows_of(1 - c)], xs.at[which, 0]
+            )
+            rest.start()
+            own.wait()
+            rest.wait()
+
+        @pl.when(far)
+        def _guest():
+            weight(which, close).wait_recv()
+            relay(which, close, 0, sibling).start()
+            weight(which, other).wait_recv()
+            stage(which, x)
+
+    def gather_remote(which):
+        weight(which, remote_band).wait_recv()
+        relay(which, remote_band, 1, sibling).start()
+
+        @pl.when(near)
+        def _home():
+            relay(which, remote_band, 0, device(1 - m, x, c)).start()
+
+        weight(which, 2 * (1 - x) + 1 - c).wait_recv()
+        stage(which, 1 - x)
+
+    def level_of(slot):
+        return same * (c * home + slot) + (1 - same) * (2 * home + c * guest + slot)
+
+    def target_of(step):
+        column = (1 - x) + (step // 2) * (2 * x - 1)
+        core = step // 2 * (1 - c) + step % 2 * (1 + step // 2 * (2 * c - 2))
+        return column, core
+
+    def give_result(slot, step):
+        column, core = target_of(step)
+        return remote(
+            fields.at[slot, band_of(column * 2 + core)], out.at[level_of(slot)],
+            bs.at[slot, step], br.at[level_of(slot)], device(x, column, core),
+        )
+
+    def own_result(slot):
+        return pltpu.make_async_copy(
+            fields.at[slot, band_of(me)], out.at[c * home + slot], bo.at[slot]
+        )
+
+    def result(level):
+        return taken(out.at[level], br.at[level])
+
+    barrier = pltpu.get_barrier_semaphore()
+    others = [device(m, x, 1 - c)]
+    others += [device(row, column, core) for row, column in ((m, 1 - x), (1 - m, x), (1 - m, 1 - x)) for core in range(2)]
+    for other in others:
+        pl.semaphore_signal(barrier, inc=1, device_id=other, device_id_type=MESH)
+    pl.semaphore_wait(barrier, len(others))
+
+    @pl.when(far)
+    def _start_far():
+        across = [(band * coeffs, far_home(0, core)) for core in (c, 1 - c)]
+        across += [(rows * cells, give(which, 0, device(m, 1 - x, c))) for which in range(2)]
+        across += [((band - SHARED * piece) * coeffs, far_tail(core)) for core in (c, 1 - c)]
+        for slot in range(home):
+            if slot not in (0, EARLY):
+                across += [(band * coeffs, far_home(slot, core)) for core in (c, 1 - c)]
+        along = [(piece * coeffs, far_piece(number)) for number in range(guests + 2 * SHARED)]
+        order = []
+        for line, entries in enumerate((along, across)):
+            begin = 0
+            for size, copy in entries:
+                order.append((begin, line, copy))
+                begin += size
+        for _, _, copy in sorted(order, key=lambda entry: entry[:2]):
+            copy.start()
+
+    @pl.when(near)
+    def _start_near():
+        for which in range(2):
+            give(which, 1, device(1 - m, x, c)).start()
+            give(which, 0, sibling).start()
+        for slot in range(home):
+            near_sibling(slot).start()
+            near_own(slot).start()
+
+    seeded = [
+        pltpu.make_async_copy(source, target, ss.at[1 + number])
+        for number, (source, target) in enumerate(
+            ((seed_cr, coarse_r), (seed_fr, fine_r), (seed_cl, coarse_l), (seed_fl, fine_l))
+        )
+    ]
+    for copy in seeded:
+        copy.start()
+    for copy in seeded:
+        copy.wait()
+
+    def rows_table(block):
+        one, at = pl.ds(block, 1), pl.ds(pl.multiple_of(block * ROWS, ROWS), ROWS)
+        cos_u, sin_u = coarse_r[0, one, :], coarse_r[1, one, :]
+        cos_v, sin_v = fine_r[0], fine_r[1]
+        high, low = split(cos_u * cos_v - sin_u * sin_v)
+        basis_h[at, :half], basis_l[at, :half] = high, low
+        high, low = split(sin_u * cos_v + cos_u * sin_v)
+        basis_h[at, half:], basis_l[at, half:] = high, low
+
+    chunk = half // 8
+
+    def lanes_table(block):
+        at = pl.ds(pl.multiple_of(block * chunk, chunk), chunk)
+        below = pl.ds(pl.multiple_of(half + block * chunk, chunk), chunk)
+        cos_v, sin_v = fine_l[0, at, :], fine_l[1, at, :]
+        cos_w, sin_w = coarse_l[0, at, :], coarse_l[1, at, :]
+        for word in range(cells // LANES):
+            lanes = slice(word * LANES, (word + 1) * LANES)
+            cos_u, sin_u = cos_w[:, word : word + 1], sin_w[:, word : word + 1]
+            high, low = split(cos_u * cos_v - sin_u * sin_v)
+            basis_th[at, lanes], basis_tl[at, lanes] = high, low
+            high, low = split(sin_u * cos_v + cos_u * sin_v)
+            basis_th[below, lanes], basis_tl[below, lanes] = high, low
+
+    blocks = cells // ROWS // 8
+
+    def build(index, _):
+        @pl.when(index < guests // 2 - 1)
+        def _send():
+            forward_guest(index)
+
+        def row(number, _):
+            rows_table(index * blocks + number)
+            return _
+
+        lax.fori_loop(0, blocks, row, 0)
+        lanes_table(index)
+        return _
+
+    lax.fori_loop(0, 8, build, 0)
+    def forward_next(number, last):
+        @pl.when((number < guests) & (number < last))
+        def _send():
+            forward_guest(number)
+
+        @pl.when((number >= guests) & (number < last))
+        def _send_home():
+            forward_home(number - guests)
+
+    def turn(which, column, factor, number, last):
+        def one(index, _):
+            forward_next(number + index, last)
+            at = pl.ds(pl.multiple_of(index * LANES, LANES), LANES)
+            to = pl.ds(pl.multiple_of(column * 2 * rows + index * LANES, LANES), LANES)
+            value = staged[at, :].T
+            turned[which, :, to] = value * factor if which == 0 else value
+            return _
+
+        lax.fori_loop(0, 2 * rows // LANES, one, 0)
+
+    pieces = guests + 2 * SHARED
+    gather_close(0)
+    turn(0, x, 1.0 / half, 7, 9)
+    gather_close(1)
+    turn(1, x, 1.0, 9, 11)
+
+    def factor(index):
+        wave = jnp.where(index < half, index, index - half)
+        return jnp.where(wave == 0, 1.0, 2.0) / cells
+
+    def tile(index):
+        return pl.ds(pl.multiple_of(index * TILE, TILE), TILE)
+
+    def one_level(slot, first):
+        take_fields(slot)
+
+        def split_field(index, _):
+            at = band_of(index)
+            wide_h[at, :coeffs], wide_l[at, :coeffs] = split(fields[slot, at, :])
+            return _
+
+        lax.fori_loop(0, coeffs // band, split_field, 0)
+
+        def synth_x(index, _):
+            if first:
+                forward_next(11 + index, 14)
+            at = tile(index)
+            value = dot3(
+                basis_h[at, :], basis_l[at, :], wide_h[:coeffs, :coeffs], wide_l[:coeffs, :coeffs]
+            )
+            side_h[at, :coeffs], side_l[at, :coeffs] = split(value)
+            return _
+
+        steps = cells // TILE
+        lax.fori_loop(0, steps, synth_x, 0)
+        if first:
+            gather_remote(0)
+            turn(0, 1 - x, 1.0 / half, 14, 16)
+        total[...] = jnp.zeros_like(total)
+
+        def synth_y(index, _):
+            if first:
+                @pl.when(index >= steps // 2)
+                def _send():
+                    forward_next(16 - steps // 2 + index, 18)
+
+            at = tile(index)
+            value = dot3(side_h[at, :coeffs], side_l[at, :coeffs], basis_th[...], basis_tl[...])
+            value = value * turned[0, at, :]
+            product[at, :] = value
+            total[...] += jnp.sum((value * value).reshape(TILE // 8, 8, cells), axis=0)
+            return _
+
+        lax.fori_loop(0, steps, synth_y, 0)
+        if first:
+            gather_remote(1)
+
+            @pl.when(near)
+            def _start_guest():
+                for other in range(guest):
+                    for core in range(2):
+                        near_guest(other, core).start()
+
+            turn(1, 1 - x, 1.0, 0, 0)
+        energy = jnp.sum(jnp.sum(total[...], axis=0, keepdims=True), axis=1, keepdims=True)
+        scale = 1.0 / jnp.sqrt(energy * (1.0 / (cells * cells)) + 1e-06)
+
+        def nonlinear(index, _):
+            if first:
+                forward_next(18 + index, pieces)
+            at = tile(index)
+            scaled = product[at, :] * scale
+            wide_h[at, :], wide_l[at, :] = split(scaled + turned[1, at, :] * scaled * scaled)
+            return _
+
+        lax.fori_loop(0, steps, nonlinear, 0)
+
+        columns = factor(lax.broadcasted_iota(jnp.int32, (1, coeffs), 1)) * half
+
+        def analyse(side, _):
+            column, _unused = target_of(2 * side)
+            at = pl.ds(pl.multiple_of(column * half, half), half)
+            value = dot3(basis_th[at, :], basis_tl[at, :], wide_h[...], wide_l[...])
+            side_h[at, :], side_l[at, :] = split(value)
+
+            def analyse_y(step, _):
+                column, core = target_of(step)
+                index = column * 2 + core
+                at = band_of(index)
+                value = dot3(side_h[at, :], side_l[at, :], basis_h[...], basis_l[...])
+                line = factor(lax.broadcasted_iota(jnp.int32, (band, 1), 0) + index * band)
+                fields[slot, at, :] = value * (line * columns)
+
+                @pl.when(step > 0)
+                def _send():
+                    give_result(slot, step - 1).start()
+
+                return _
+
+            lax.fori_loop(2 * side, 2 * side + 2, analyse_y, 0)
+
+            return _
+
+        lax.fori_loop(0, 2, analyse, 0)
+
+        @pl.when(near)
+        def _keep():
+            own_result(slot).start()
+
+        @pl.when(far)
+        def _last():
+            give_result(slot, 3).start()
+
+    one_level(0, True)
+
+    def later(slot, _):
+        one_level(slot, False)
+        return _
+
+    lax.fori_loop(1, guest + same * (home - guest), later, 0)
+
+    @pl.when(near)
+    def _finish_near():
+        for which in range(2):
+            give(which, 1, sibling).wait_send()
+            give(which, 0, sibling).wait_send()
+            relay(which, remote_band, 0, sibling).wait_send()
+            relay(which, remote_band, 1, sibling).wait_send()
+        for slot in range(guest):
+            for core in range(2):
+                near_guest(slot, core).wait_send()
+
+        def sent(number, _):
+            forwarded(number).wait_send()
+            return _
+
+        lax.fori_loop(0, guests + 2 * SHARED, sent, 0)
+
+        def done(slot, _):
+            near_sibling(slot).wait_send()
+            for step in range(3):
+                give_result(slot, step).wait_send()
+            own_result(slot).wait()
+            result((1 - c) * home + slot).wait_recv()
+            return _
+
+        lax.fori_loop(0, home, done, 0)
+        for number in range(2 * guest):
+            result(2 * home + number).wait_recv()
+
+    @pl.when(far)
+    def _finish_far():
+        for which in range(2):
+            give(which, 0, sibling).wait_send()
+            relay(which, close, 0, sibling).wait_send()
+            relay(which, remote_band, 1, sibling).wait_send()
+
+        def sent(number, _):
+            far_piece_landed(number).wait_send()
+            return _
+
+        lax.fori_loop(0, guests + 2 * SHARED, sent, 0)
+        for slot in range(home):
+            for core in range(2):
+                if slot != EARLY:
+                    far_home(slot, core).wait_send()
+        for core in range(2):
+            far_tail(core).wait_send()
+        for slot in range(guest):
+            for step in range(4):
+                give_result(slot, step).wait_send()
+
+        def done(level, _):
+            result(level).wait_recv()
+            return _
+
+        lax.fori_loop(0, levels, done, 0)
+
+
+def on_pairs(spectral, coupling, quadratic):
+    levels, band, coeffs = spectral.shape
+    rows, cells = coupling.shape
+    home, guest = levels * 3 // 8, levels // 8
+    pieces = 2 * guest * PIECES + 2 * SHARED
+    away = pl.BlockSpec(memory_space=pltpu.HBM)
+    inside = pl.BlockSpec(memory_space=pltpu.VMEM)
+    tables = seeds(cells, coeffs)
+    copies = pltpu.SemaphoreType.DMA
+    return pl.pallas_call(
+        paired,
+        out_shape=(
+            pltpu.VMEM((levels, band, coeffs), F32),
+            pltpu.HBM((2, cells, cells), F32),
+        ),
+        in_specs=[away] * 7,
+        out_specs=(inside, away),
+        scratch_shapes=[
+            *(pltpu.VMEM(table.shape, F32) for table in tables),
+            pltpu.VMEM((home, coeffs, coeffs), F32),
+            pltpu.VMEM((pieces, band // PIECES, coeffs), F32),
+            pltpu.VMEM((2, cells, cells), F32),
+            pltpu.VMEM((cells, coeffs), BF16),
+            pltpu.VMEM((cells, coeffs), BF16),
+            pltpu.VMEM((coeffs, cells), BF16),
+            pltpu.VMEM((coeffs, cells), BF16),
+            pltpu.VMEM((cells, cells), BF16),
+            pltpu.VMEM((cells, cells), BF16),
+            pltpu.VMEM((cells, cells), BF16),
+            pltpu.VMEM((cells, cells), BF16),
+            pltpu.VMEM((cells, cells), F32),
+            pltpu.VMEM((2 * rows, cells), F32),
+            pltpu.VMEM((8, cells), F32),
+            copies((1 + len(tables),)),
+            copies((home, 2)),
+            copies((home, 4)),
+            copies((home,)),
+            copies((guest, 2)),
+            copies((pieces,)),
+            copies((pieces,)),
+            copies((pieces,)),
+            copies((pieces, 2)),
+            copies((2, 2)),
+            copies((2, 4)),
+            copies((2,)),
+            copies((2, 2)),
+            copies((2, 2)),
+            copies((home, 4)),
+            copies((levels,)),
+            copies((home,)),
+        ],
+        compiler_params=pltpu.CompilerParams(
+            collective_id=1, has_side_effects=True, vmem_limit_bytes=53 * 2**20
+        ),
+        name="paired",
+    )(spectral, coupling, quadratic, *tables)[0]
+
+
 def solution(mesh):
     placed = (P("member", "band", None), P(("member", "band"), None), P(("member", "band"), None))
+    pairs = mesh.shape["band"] == 4 and mesh.shape["member"] % 2 == 0
     return jax.shard_map(
-        on_device, mesh=mesh, in_specs=placed, out_specs=P("member", "band", None), check_vma=False
+        on_pairs if pairs else on_device,
+        mesh=mesh,
+        in_specs=placed,
+        out_specs=P("member", "band", None),
+        check_vma=False,
     )

time: 257 us -> 245 us (0.953)
  Pallas kernels: 253 us -> 241 us
    pallas_call x1, Pallas kernels: 253 us -> 241 us  [on_pairs(): pl.pallas_call(paired, out_shape=(pltpu.VMEM((levels, band, coeffs), F32)...]
where the time goes in v3:
time: 245 us
  Pallas kernels  241 us (98%)
  local copies, waits for them, and re-layouts  3.74 us (2%)
    pallas_call x1, Pallas kernels, on_pairs(): pl.pallas_call(paired, out_shape=(pltpu.VMEM((levels, band, coeffs), F32)...  241 us

profile of v3, /device:TPU:0, one launch (start us, length us, event | category | flops | bytes accessed | tf_op | source)
XLA Modules:
  0.0 244.9 jit_solution(13472180331209955441)
XLA Ops:
  0.0 241.1 %paired.1 = (f32[16,192,768]{2,1,0:T(8,128)S(1)}, f32[2,1024,1024]{2,1,0:T(8,128)}) custom-call(f32[16,192,768]{2,1,0:T(8,128)} %spectral.1, f32[256,1024]{1,0:T(8,128)} %coupling.1, f32[256,1024]{1,0:T(8,128)} %quadratic.1, f32[2,32,384]{2,1,0:T(8,128)} %constant.8.clone.seed_cr, f32[2,32,384]{2,1,0:T(8,128)} %constant.9.clone.seed_fr, ...), custom_call_target="tpu_custom_call" | custom-call | tf_op jit(solution)/shard_map/paired/pallas_call | solution.py:914
  241.1 3.7 %copy.9 = f32[16,192,768]{2,1,0:T(8,128)} copy(f32[16,192,768]{2,1,0:T(8,128)S(1)} %get-tuple-element.6) | data formatting | bytes 18874368
